TPU v7x, 256 devices: a whole 4x4x8 slice. The times are simulated.
256 devices in a mesh: dp: 8 (over x, core), band: 32 (over y, z).
Axes of the slice: x: 4, y: 4, z: 8, core: 2. Of those that a mesh axis runs over, the one named last changes fastest.
Arguments:
- features: bfloat16 [65280, 256], P(('dp', 'band')), parts along dimension 0, may hold values from -6 to 6
- corners: int32 [65280, 512], P(('dp', 'band')), parts along dimension 0, may hold values from 0 to 6143, as said below
- bilinear: float32 [65280, 512], P(('dp', 'band')), parts along dimension 0, may hold values from 0.08 to 0.5, as said below
- attention: float32 [65280, 128], P(('dp', 'band')), parts along dimension 0, may hold values from 0 to 1, as said below
- w_value: bfloat16 [256, 256], replicated, may hold values from -0.375 to 0.375
- b_value: float32 [256], replicated, may hold values from -0.6 to 0.6
- w_out: bfloat16 [256, 256], replicated, may hold values from -1.5 to 1.5
- b_out: float32 [256], replicated, may hold values from -3 to 3
- norm1_gain: float32 [256], replicated, may hold values from 0.5 to 1.5
- norm1_bias: float32 [256], replicated, may hold values from -3 to 3
- w_in: bfloat16 [256, 1024], replicated, may hold values from -0.375 to 0.375
- b_in: float32 [1024], replicated, may hold values from -3 to 3
- w_ffout: bfloat16 [1024, 256], replicated, may hold values from -0.1875 to 0.1875
- b_ffout: float32 [256], replicated, may hold values from -3 to 3
- norm2_gain: float32 [256], replicated, may hold values from 0.5 to 1.5
- norm2_bias: float32 [256], replicated, may hold values from -3 to 3
Outputs:
- encoded: bfloat16 [65280, 256], P(('dp', 'band')), parts along dimension 0
There are 8 independent parts, one for each index of `dp`. A program takes and returns all parts, laid end to end along the dimension named above; an argument that names none is the same for every part. Nothing has to cross between parts.
Inputs may be any that keep to these rules, and one draw needn't show every extreme that they name: An entry for level l is a row of a map of 192 * 32 // 4**l tokens laid out in rows of 128 // 2**l; the four corners of a point are k, k + 1, k + 128 // 2**l and k + 128 // 2**l + 1 in that order. `bilinear`: the four corner weights of a point are positive and sum to one. `attention`: for each token and head the 16 weights are positive and sum to one.
All inputs are finite; a program needn't handle non-finite values.
Results may differ from a plain program's by a relative error of at most 0.009.
Values may be sent and summed in bfloat16 or wider, within the bound.
A program may use at most 64 MiB of HBM per device.

v0:
```python
import jax
import jax.numpy as jnp
from jax import lax
from jax.sharding import Mesh
from jax.sharding import PartitionSpec as P

HEADS = 8
LEVELS = 4
POINTS = 4
ROWS_DEV = 192
BAND = ("band_0", "band_1")
DP_BAND = ("dp", "band_0", "band_1")


def joined_along(pieces, dim):
    pieces = jnp.moveaxis(pieces, 0, dim)
    dims = pieces.shape
    return pieces.reshape(*dims[:dim], dims[dim] * dims[dim + 1], *dims[dim + 2 :])


def stacked_from(shard, axes, order):
    pieces = shard[None]
    for k in order:
        pieces = lax.all_gather(pieces, axes[k], axis=0, tiled=True)
    held = [lax.axis_size(axes[k]) for k in reversed(order)]
    pieces = pieces.reshape(*held, *shard.shape)
    turned = sorted(range(len(order)), key=lambda place: order[len(order) - 1 - place])
    return pieces.transpose(*turned, *range(len(order), pieces.ndim)).reshape(-1, *shard.shape)


def gathered_by_axis(shard, axes, order, dim):
    return joined_along(stacked_from(shard, axes, order), dim)


def layer_norm(inputs, gain, shift):
    average = jnp.mean(inputs, axis=-1, keepdims=True)
    centred = inputs - average
    variance = jnp.mean(centred * centred, axis=-1, keepdims=True)
    return centred * lax.rsqrt(variance + 1e-05) * gain + shift


def blend_rows(place_heads, weight_heads, value_block):
    row_count, model_width = value_block.shape
    head_dim = model_width // HEADS
    lane_groups = -(-row_count // 128)
    padding = lane_groups * 128 - row_count
    padded = jnp.pad(value_block, ((0, padding), (0, 0))).reshape(lane_groups, 128, HEADS, head_dim)
    per_head = jnp.transpose(padded, (2, 0, 1, 3))
    group_ids = jnp.arange(lane_groups, dtype=jnp.int32)
    lane_ids = jnp.arange(128, dtype=jnp.int32)

    def one_head(head_args):
        place_one, weight_one, value_one = head_args
        group_index = place_one // 128
        lane_index = place_one % 128
        group_hits = jnp.where(
            group_index[..., None] == group_ids, weight_one[..., None], jnp.zeros((), jnp.bfloat16)
        )
        lane_hits = (lane_index[..., None] == lane_ids).astype(jnp.bfloat16)
        hit_table = jnp.einsum(
            "qsa,qsb->qab", group_hits, lane_hits, preferred_element_type=jnp.float32
        )
        table_major = hit_table.astype(jnp.bfloat16)
        table_minor = (hit_table - table_major.astype(jnp.float32)).astype(jnp.bfloat16)
        result_major = jnp.einsum(
            "qab,abd->qd", table_major, value_one, preferred_element_type=jnp.float32
        )
        result_minor = jnp.einsum(
            "qab,abd->qd", table_minor, value_one, preferred_element_type=jnp.float32
        )
        return result_major + result_minor

    blended = lax.map(one_head, (place_heads, weight_heads, per_head))
    return jnp.transpose(blended, (1, 0, 2))


def body(
    features,
    corners,
    bilinear,
    attention,
    w_value,
    b_value,
    w_out,
    b_out,
    norm1_gain,
    norm1_bias,
    w_in,
    b_in,
    w_ffout,
    b_ffout,
    norm2_gain,
    norm2_bias,
):
    band_rows, model_width = features.shape
    samples = LEVELS * POINTS * 4
    segment_rows = [ROWS_DEV // 4**level_index for level_index in range(LEVELS)]
    segment_start = [sum(segment_rows[:level_index]) for level_index in range(LEVELS)]
    value_rows = (jnp.dot(features, w_value, preferred_element_type=jnp.float32) + b_value).astype(
        jnp.bfloat16
    )
    weight = (
        attention.reshape(band_rows, HEADS, LEVELS, POINTS, 1)
        * bilinear.reshape(band_rows, HEADS, LEVELS, POINTS, 4)
    ).astype(jnp.bfloat16)
    weight_heads = jnp.transpose(weight.reshape(band_rows, HEADS, samples), (1, 0, 2))
    corner_table = corners.reshape(band_rows, HEADS, LEVELS, POINTS * 4)
    places = []
    for level_index in range(LEVELS):
        level_corner = corner_table[:, :, level_index]
        places.append(
            level_corner // segment_rows[level_index] * band_rows
            + segment_start[level_index]
            + level_corner % segment_rows[level_index]
        )
    place_table = jnp.stack(places, axis=2).reshape(band_rows, HEADS, samples)
    place_heads = jnp.transpose(place_table, (1, 0, 2))
    whole = gathered_by_axis(value_rows, BAND, (0, 1), 0)
    running_sum = blend_rows(place_heads, weight_heads, whole)
    sampled = running_sum.reshape(band_rows, model_width).astype(jnp.bfloat16)
    attended = jnp.dot(sampled, w_out, preferred_element_type=jnp.float32) + b_out
    middle = layer_norm(features.astype(jnp.float32) + attended, norm1_gain, norm1_bias).astype(
        jnp.bfloat16
    )
    hidden = jnp.maximum(
        jnp.dot(middle, w_in, preferred_element_type=jnp.float32) + b_in, 0.0
    ).astype(jnp.bfloat16)
    result = (
        middle.astype(jnp.float32)
        + jnp.dot(hidden, w_ffout, preferred_element_type=jnp.float32)
        + b_ffout
    )
    return layer_norm(result, norm2_gain, norm2_bias).astype(jnp.bfloat16)


def solution(mesh):
    split = Mesh(mesh.devices.reshape(mesh.shape["dp"], 4, 8), ("dp", "band_0", "band_1"))
    return jax.shard_map(
        body,
        mesh=split,
        in_specs=(
            P(DP_BAND, None),
            P(DP_BAND, None),
            P(DP_BAND, None),
            P(DP_BAND, None),
            P(),
            P(),
            P(),
            P(),
            P(),
            P(),
            P(),
            P(),
            P(),
            P(),
            P(),
            P(),
        ),
        out_specs=P(DP_BAND, None),
        check_vma=False,
    )
```

profile of v0, /device:TPU:1, one launch (start us, length us, event | category | flops | bytes accessed | tf_op | source)
XLA Modules:
  0.0 196.2 jit_solution(10287885254114032804)
XLA Ops:
  6.5 1.2 fusion.41
  7.8 13.0 %all-gather.1 = bf16[4,255,256]{2,1,0:T(8,128)(2,1)} all-gather(bf16[1,255,256]{2,1,0:T(8,128)(2,1)S(1)} %fusion.41), channel_id=2, replica_groups=mesh['dp'=8,'band_0'=4,'band_1'=8] {'band_0'}, dimensions={0}, use_global_device_ids=true | all-gather | bytes 652800 | tf_op jit(solution)/shard_map/all_gather | solution.py:24
  20.8 1.2 copy.38
  22.0 1.2 copy.41
  23.3 1.0 copy.39
  24.7 0.5 fusion.46
  25.3 55.0 %all-gather.4.cloned.1.call-done = bf16[32,255,256]{2,1,0:T(8,128)(2,1)} async-done(((bf16[4,255,256]{2,1,0:T(8,128)(2,1)}), bf16[32,255,256]{2,1,0:T(8,128)(2,1)}) %all-gather.4.cloned.1.call-update) | async-done | bytes 4177936 | tf_op jit(solution)/shard_map/all_gather | solution.py:24
  80.3 4.6 %copy.72 = bf16[8,4,255,256]{3,2,0,1:T(8,128)(2,1)} copy(bf16[8,4,255,256]{3,2,1,0:T(8,128)(2,1)} %bitcast.96) | data formatting | bytes 8355840 | tf_op jit(solution)/shard_map/reshape | solution.py:26
  84.9 5.2 %reshape_reshape.3 = bf16[8160,256]{1,0:T(8,128)(2,1)} reshape(bf16[4,8,255,256]{3,2,1,0:T(8,128)(2,1)} %bitcast.94) | data formatting | bytes 8355840 | tf_op jit(solution)/shard_map/reshape;reshape | solution.py:18
  90.1 6.4 %copy.51 = bf16[8160,256]{0,1:T(8,128)(2,1)} copy(bf16[8160,256]{1,0:T(8,128)(2,1)} %reshape_reshape.3) | data formatting | bytes 8355840
  96.5 2.5 %pad_bitcast_fusion = bf16[32,8,64,128]{3,1,2,0:T(8,128)(2,1)S(1)} fusion(bf16[8160,256]{0,1:T(8,128)(2,1)} %copy.51), kind=kLoop, calls=%fused_computation.35 | loop fusion | bytes 8372224
  99.0 3.1 %copy.52 = bf16[32,8,64,128]{3,2,1,0:T(8,128)(2,1)} copy(bf16[32,8,64,128]{3,1,2,0:T(8,128)(2,1)S(1)} %pad_bitcast_fusion) | data formatting | bytes 8388608
  102.2 84.8 %while.13 = (s32[]{:T(128)}, bf16[8,255,32]{1,2,0:T(8,128)(2,1)S(1)}, s32[8,255,64]{1,2,0:T(8,128)S(1)}, bf16[8,255,64]{1,0,2:T(8,128)(2,1)S(1)}, bf16[8,64,128,32]{2,1,3,0:T(8,128)(2,1)}, /*index=5*/s32[]{:T(128)}) while((s32[]{:T(128)}, bf16[8,255,32]{1,2,0:T(8,128)(2,1)S(1)}, s32[8,255,64]{1,2,0:T(8,128)S(1)}, ...), condition=%wide.region_1.2_spmd.clone, body=%wide.region_0.1_spmd.clone.sunk | while | flops 547625728 | bytes 19657812 | solution.py:73
  102.7 3.9 %subtract_convert_fusion.2 = (bf16[255,64,128]{2,1,0:T(8,128)(2,1)S(1)}, bf16[255,64,128]{2,1,0:T(8,128)(2,1)S(1)}) fusion(s32[255,64]{1,0:T(8,128)S(1)} %get-tuple-element.178, s32[255,64]{1,0:T(8,128)S(1)} %get-tuple-element.179, bf16[255,64]{1,0:T(8,128)(2,1)S(1)} %bitcast.99), kind=kOutput, calls=%fused_computation.4.clone.1 | convolution fusion | flops 279920640 | bytes 8519040 | tf_op jit(solution)/shard_map/while/body/eval_jaxpr/qsa,qsb->qab/dot_general | solution.py:60
  106.6 1.1 constant_dynamic-slice_fusion.8
  107.7 2.5 %fusion.83 = f32[255,32]{0,1:T(8,128)S(1)} fusion(bf16[255,64,128]{2,1,0:T(8,128)(2,1)S(1)} %get-tuple-element.180, bf16[1,64,128,32]{2,1,3,0:T(8,128)(2,1)S(1)} %constant_dynamic-slice_fusion.8), kind=kOutput, calls=%fused_computation.15.clone.1 | convolution fusion | flops 133693440 | bytes 4734848 | tf_op jit(solution)/shard_map/while/body/eval_jaxpr/qab,abd->qd/dot_general | solution.py:65
  110.3 2.5 %fusion.84 = bf16[8,255,32]{1,2,0:T(8,128)(2,1)S(1)} fusion(bf16[8,255,32]{1,2,0:T(8,128)(2,1)S(1)} %get-tuple-element.189, s32[]{:T(128)} %get-tuple-element.188, f32[255,32]{0,1:T(8,128)S(1)} %fusion.83, bf16[255,64,128]{2,1,0:T(8,128)(2,1)S(1)} %get-tuple-element.181, bf16[1,64,128,32]{2,1,3,0:T(8,128)(2,1)S(1)} %constant_dynamic-slice_fusion.8), kind=kOutput, calls=%fused_computation.19.clone.1 | convolution fusion | flops 133701600 | bytes 4767748 | tf_op jit(solution)/shard_map/while/body/eval_jaxpr/qab,abd->qd/dot_general | solution.py:68
  113.3 4.0 %subtract_convert_fusion.2 = (bf16[255,64,128]{2,1,0:T(8,128)(2,1)S(1)}, bf16[255,64,128]{2,1,0:T(8,128)(2,1)S(1)}) fusion(s32[255,64]{1,0:T(8,128)S(1)} %get-tuple-element.178, s32[255,64]{1,0:T(8,128)S(1)} %get-tuple-element.179, bf16[255,64]{1,0:T(8,128)(2,1)S(1)} %bitcast.99), kind=kOutput, calls=%fused_computation.4.clone.1 | convolution fusion | flops 279920640 | bytes 8519040 | tf_op jit(solution)/shard_map/while/body/eval_jaxpr/qsa,qsb->qab/dot_general | solution.py:60
  117.2 1.1 constant_dynamic-slice_fusion.8
  118.3 2.5 %fusion.83 = f32[255,32]{0,1:T(8,128)S(1)} fusion(bf16[255,64,128]{2,1,0:T(8,128)(2,1)S(1)} %get-tuple-element.180, bf16[1,64,128,32]{2,1,3,0:T(8,128)(2,1)S(1)} %constant_dynamic-slice_fusion.8), kind=kOutput, calls=%fused_computation.15.clone.1 | convolution fusion | flops 133693440 | bytes 4734848 | tf_op jit(solution)/shard_map/while/body/eval_jaxpr/qab,abd->qd/dot_general | solution.py:65
  120.9 2.5 %fusion.84 = bf16[8,255,32]{1,2,0:T(8,128)(2,1)S(1)} fusion(bf16[8,255,32]{1,2,0:T(8,128)(2,1)S(1)} %get-tuple-element.189, s32[]{:T(128)} %get-tuple-element.188, f32[255,32]{0,1:T(8,128)S(1)} %fusion.83, bf16[255,64,128]{2,1,0:T(8,128)(2,1)S(1)} %get-tuple-element.181, bf16[1,64,128,32]{2,1,3,0:T(8,128)(2,1)S(1)} %constant_dynamic-slice_fusion.8), kind=kOutput, calls=%fused_computation.19.clone.1 | convolution fusion | flops 133701600 | bytes 4767748 | tf_op jit(solution)/shard_map/while/body/eval_jaxpr/qab,abd->qd/dot_general | solution.py:68
  123.9 3.9 %subtract_convert_fusion.2 = (bf16[255,64,128]{2,1,0:T(8,128)(2,1)S(1)}, bf16[255,64,128]{2,1,0:T(8,128)(2,1)S(1)}) fusion(s32[255,64]{1,0:T(8,128)S(1)} %get-tuple-element.178, s32[255,64]{1,0:T(8,128)S(1)} %get-tuple-element.179, bf16[255,64]{1,0:T(8,128)(2,1)S(1)} %bitcast.99), kind=kOutput, calls=%fused_computation.4.clone.1 | convolution fusion | flops 279920640 | bytes 8519040 | tf_op jit(solution)/shard_map/while/body/eval_jaxpr/qsa,qsb->qab/dot_general | solution.py:60
  127.8 1.1 constant_dynamic-slice_fusion.8
  128.9 2.5 %fusion.83 = f32[255,32]{0,1:T(8,128)S(1)} fusion(bf16[255,64,128]{2,1,0:T(8,128)(2,1)S(1)} %get-tuple-element.180, bf16[1,64,128,32]{2,1,3,0:T(8,128)(2,1)S(1)} %constant_dynamic-slice_fusion.8), kind=kOutput, calls=%fused_computation.15.clone.1 | convolution fusion | flops 133693440 | bytes 4734848 | tf_op jit(solution)/shard_map/while/body/eval_jaxpr/qab,abd->qd/dot_general | solution.py:65
  131.5 2.5 %fusion.84 = bf16[8,255,32]{1,2,0:T(8,128)(2,1)S(1)} fusion(bf16[8,255,32]{1,2,0:T(8,128)(2,1)S(1)} %get-tuple-element.189, s32[]{:T(128)} %get-tuple-element.188, f32[255,32]{0,1:T(8,128)S(1)} %fusion.83, bf16[255,64,128]{2,1,0:T(8,128)(2,1)S(1)} %get-tuple-element.181, bf16[1,64,128,32]{2,1,3,0:T(8,128)(2,1)S(1)} %constant_dynamic-slice_fusion.8), kind=kOutput, calls=%fused_computation.19.clone.1 | convolution fusion | flops 133701600 | bytes 4767748 | tf_op jit(solution)/shard_map/while/body/eval_jaxpr/qab,abd->qd/dot_general | solution.py:68
  134.5 4.0 %subtract_convert_fusion.2 = (bf16[255,64,128]{2,1,0:T(8,128)(2,1)S(1)}, bf16[255,64,128]{2,1,0:T(8,128)(2,1)S(1)}) fusion(s32[255,64]{1,0:T(8,128)S(1)} %get-tuple-element.178, s32[255,64]{1,0:T(8,128)S(1)} %get-tuple-element.179, bf16[255,64]{1,0:T(8,128)(2,1)S(1)} %bitcast.99), kind=kOutput, calls=%fused_computation.4.clone.1 | convolution fusion | flops 279920640 | bytes 8519040 | tf_op jit(solution)/shard_map/while/body/eval_jaxpr/qsa,qsb->qab/dot_general | solution.py:60
  138.4 1.1 constant_dynamic-slice_fusion.8
  139.5 2.5 %fusion.83 = f32[255,32]{0,1:T(8,128)S(1)} fusion(bf16[255,64,128]{2,1,0:T(8,128)(2,1)S(1)} %get-tuple-element.180, bf16[1,64,128,32]{2,1,3,0:T(8,128)(2,1)S(1)} %constant_dynamic-slice_fusion.8), kind=kOutput, calls=%fused_computation.15.clone.1 | convolution fusion | flops 133693440 | bytes 4734848 | tf_op jit(solution)/shard_map/while/body/eval_jaxpr/qab,abd->qd/dot_general | solution.py:65
  142.1 2.5 %fusion.84 = bf16[8,255,32]{1,2,0:T(8,128)(2,1)S(1)} fusion(bf16[8,255,32]{1,2,0:T(8,128)(2,1)S(1)} %get-tuple-element.189, s32[]{:T(128)} %get-tuple-element.188, f32[255,32]{0,1:T(8,128)S(1)} %fusion.83, bf16[255,64,128]{2,1,0:T(8,128)(2,1)S(1)} %get-tuple-element.181, bf16[1,64,128,32]{2,1,3,0:T(8,128)(2,1)S(1)} %constant_dynamic-slice_fusion.8), kind=kOutput, calls=%fused_computation.19.clone.1 | convolution fusion | flops 133701600 | bytes 4767748 | tf_op jit(solution)/shard_map/while/body/eval_jaxpr/qab,abd->qd/dot_general | solution.py:68
  145.1 4.0 %subtract_convert_fusion.2 = (bf16[255,64,128]{2,1,0:T(8,128)(2,1)S(1)}, bf16[255,64,128]{2,1,0:T(8,128)(2,1)S(1)}) fusion(s32[255,64]{1,0:T(8,128)S(1)} %get-tuple-element.178, s32[255,64]{1,0:T(8,128)S(1)} %get-tuple-element.179, bf16[255,64]{1,0:T(8,128)(2,1)S(1)} %bitcast.99), kind=kOutput, calls=%fused_computation.4.clone.1 | convolution fusion | flops 279920640 | bytes 8519040 | tf_op jit(solution)/shard_map/while/body/eval_jaxpr/qsa,qsb->qab/dot_general | solution.py:60
  149.0 1.1 constant_dynamic-slice_fusion.8
  150.1 2.5 %fusion.83 = f32[255,32]{0,1:T(8,128)S(1)} fusion(bf16[255,64,128]{2,1,0:T(8,128)(2,1)S(1)} %get-tuple-element.180, bf16[1,64,128,32]{2,1,3,0:T(8,128)(2,1)S(1)} %constant_dynamic-slice_fusion.8), kind=kOutput, calls=%fused_computation.15.clone.1 | convolution fusion | flops 133693440 | bytes 4734848 | tf_op jit(solution)/shard_map/while/body/eval_jaxpr/qab,abd->qd/dot_general | solution.py:65
  152.7 2.5 %fusion.84 = bf16[8,255,32]{1,2,0:T(8,128)(2,1)S(1)} fusion(bf16[8,255,32]{1,2,0:T(8,128)(2,1)S(1)} %get-tuple-element.189, s32[]{:T(128)} %get-tuple-element.188, f32[255,32]{0,1:T(8,128)S(1)} %fusion.83, bf16[255,64,128]{2,1,0:T(8,128)(2,1)S(1)} %get-tuple-element.181, bf16[1,64,128,32]{2,1,3,0:T(8,128)(2,1)S(1)} %constant_dynamic-slice_fusion.8), kind=kOutput, calls=%fused_computation.19.clone.1 | convolution fusion | flops 133701600 | bytes 4767748 | tf_op jit(solution)/shard_map/while/body/eval_jaxpr/qab,abd->qd/dot_general | solution.py:68
  155.7 4.0 %subtract_convert_fusion.2 = (bf16[255,64,128]{2,1,0:T(8,128)(2,1)S(1)}, bf16[255,64,128]{2,1,0:T(8,128)(2,1)S(1)}) fusion(s32[255,64]{1,0:T(8,128)S(1)} %get-tuple-element.178, s32[255,64]{1,0:T(8,128)S(1)} %get-tuple-element.179, bf16[255,64]{1,0:T(8,128)(2,1)S(1)} %bitcast.99), kind=kOutput, calls=%fused_computation.4.clone.1 | convolution fusion | flops 279920640 | bytes 8519040 | tf_op jit(solution)/shard_map/while/body/eval_jaxpr/qsa,qsb->qab/dot_general | solution.py:60
  159.6 1.1 constant_dynamic-slice_fusion.8
  160.7 2.5 %fusion.83 = f32[255,32]{0,1:T(8,128)S(1)} fusion(bf16[255,64,128]{2,1,0:T(8,128)(2,1)S(1)} %get-tuple-element.180, bf16[1,64,128,32]{2,1,3,0:T(8,128)(2,1)S(1)} %constant_dynamic-slice_fusion.8), kind=kOutput, calls=%fused_computation.15.clone.1 | convolution fusion | flops 133693440 | bytes 4734848 | tf_op jit(solution)/shard_map/while/body/eval_jaxpr/qab,abd->qd/dot_general | solution.py:65
  163.3 2.5 %fusion.84 = bf16[8,255,32]{1,2,0:T(8,128)(2,1)S(1)} fusion(bf16[8,255,32]{1,2,0:T(8,128)(2,1)S(1)} %get-tuple-element.189, s32[]{:T(128)} %get-tuple-element.188, f32[255,32]{0,1:T(8,128)S(1)} %fusion.83, bf16[255,64,128]{2,1,0:T(8,128)(2,1)S(1)} %get-tuple-element.181, bf16[1,64,128,32]{2,1,3,0:T(8,128)(2,1)S(1)} %constant_dynamic-slice_fusion.8), kind=kOutput, calls=%fused_computation.19.clone.1 | convolution fusion | flops 133701600 | bytes 4767748 | tf_op jit(solution)/shard_map/while/body/eval_jaxpr/qab,abd->qd/dot_general | solution.py:68
  166.3 3.9 %subtract_convert_fusion.2 = (bf16[255,64,128]{2,1,0:T(8,128)(2,1)S(1)}, bf16[255,64,128]{2,1,0:T(8,128)(2,1)S(1)}) fusion(s32[255,64]{1,0:T(8,128)S(1)} %get-tuple-element.178, s32[255,64]{1,0:T(8,128)S(1)} %get-tuple-element.179, bf16[255,64]{1,0:T(8,128)(2,1)S(1)} %bitcast.99), kind=kOutput, calls=%fused_computation.4.clone.1 | convolution fusion | flops 279920640 | bytes 8519040 | tf_op jit(solution)/shard_map/while/body/eval_jaxpr/qsa,qsb->qab/dot_general | solution.py:60
  170.3 1.1 constant_dynamic-slice_fusion.8
  171.3 2.5 %fusion.83 = f32[255,32]{0,1:T(8,128)S(1)} fusion(bf16[255,64,128]{2,1,0:T(8,128)(2,1)S(1)} %get-tuple-element.180, bf16[1,64,128,32]{2,1,3,0:T(8,128)(2,1)S(1)} %constant_dynamic-slice_fusion.8), kind=kOutput, calls=%fused_computation.15.clone.1 | convolution fusion | flops 133693440 | bytes 4734848 | tf_op jit(solution)/shard_map/while/body/eval_jaxpr/qab,abd->qd/dot_general | solution.py:65
  173.9 2.5 %fusion.84 = bf16[8,255,32]{1,2,0:T(8,128)(2,1)S(1)} fusion(bf16[8,255,32]{1,2,0:T(8,128)(2,1)S(1)} %get-tuple-element.189, s32[]{:T(128)} %get-tuple-element.188, f32[255,32]{0,1:T(8,128)S(1)} %fusion.83, bf16[255,64,128]{2,1,0:T(8,128)(2,1)S(1)} %get-tuple-element.181, bf16[1,64,128,32]{2,1,3,0:T(8,128)(2,1)S(1)} %constant_dynamic-slice_fusion.8), kind=kOutput, calls=%fused_computation.19.clone.1 | convolution fusion | flops 133701600 | bytes 4767748 | tf_op jit(solution)/shard_map/while/body/eval_jaxpr/qab,abd->qd/dot_general | solution.py:68
  176.9 4.0 %subtract_convert_fusion.2 = (bf16[255,64,128]{2,1,0:T(8,128)(2,1)S(1)}, bf16[255,64,128]{2,1,0:T(8,128)(2,1)S(1)}) fusion(s32[255,64]{1,0:T(8,128)S(1)} %get-tuple-element.178, s32[255,64]{1,0:T(8,128)S(1)} %get-tuple-element.179, bf16[255,64]{1,0:T(8,128)(2,1)S(1)} %bitcast.99), kind=kOutput, calls=%fused_computation.4.clone.1 | convolution fusion | flops 279920640 | bytes 8519040 | tf_op jit(solution)/shard_map/while/body/eval_jaxpr/qsa,qsb->qab/dot_general | solution.py:60
  180.9 1.1 constant_dynamic-slice_fusion.8
  181.9 2.5 %fusion.83 = f32[255,32]{0,1:T(8,128)S(1)} fusion(bf16[255,64,128]{2,1,0:T(8,128)(2,1)S(1)} %get-tuple-element.180, bf16[1,64,128,32]{2,1,3,0:T(8,128)(2,1)S(1)} %constant_dynamic-slice_fusion.8), kind=kOutput, calls=%fused_computation.15.clone.1 | convolution fusion | flops 133693440 | bytes 4734848 | tf_op jit(solution)/shard_map/while/body/eval_jaxpr/qab,abd->qd/dot_general | solution.py:65
  184.5 2.5 %fusion.84 = bf16[8,255,32]{1,2,0:T(8,128)(2,1)S(1)} fusion(bf16[8,255,32]{1,2,0:T(8,128)(2,1)S(1)} %get-tuple-element.189, s32[]{:T(128)} %get-tuple-element.188, f32[255,32]{0,1:T(8,128)S(1)} %fusion.83, bf16[255,64,128]{2,1,0:T(8,128)(2,1)S(1)} %get-tuple-element.181, bf16[1,64,128,32]{2,1,3,0:T(8,128)(2,1)S(1)} %constant_dynamic-slice_fusion.8), kind=kOutput, calls=%fused_computation.19.clone.1 | convolution fusion | flops 133701600 | bytes 4767748 | tf_op jit(solution)/shard_map/while/body/eval_jaxpr/qab,abd->qd/dot_general | solution.py:68
  187.1 0.3 fusion.69
  187.6 0.7 fusion.70
  188.5 0.8 add_convert_fusion
  (75 shorter events, 4.4 us)
Async XLA Ops:
  6.5 181.1 %copy-start = (bf16[1024,256]{1,0:T(8,128)(2,1)S(1)}, bf16[1024,256]{1,0:T(8,128)(2,1)}, u32[]{:S(2)}) copy-start(bf16[1024,256]{1,0:T(8,128)(2,1)} %param.30) | copy-start | bytes 1572868
  6.5 73.8 %all-gather.4.cloned.1.call-start = ((), (), s32[]{:S(2)}) async-start(), calls=%async_computation | async-start | bytes 4718592 | tf_op jit(solution)/shard_map/all_gather | solution.py:24
  102.1 84.9 %copy-start.1 = (bf16[255,256]{1,0:T(8,128)(2,1)S(1)}, bf16[255,256]{1,0:T(8,128)(2,1)}, u32[]{:S(2)}) copy-start(bf16[255,256]{1,0:T(8,128)(2,1)} %param.18) | copy-start | bytes 391684
  102.1 84.9 %copy-start.2 = (bf16[256,256]{1,0:T(8,128)(2,1)S(1)}, bf16[256,256]{1,0:T(8,128)(2,1)}, u32[]{:S(2)}) copy-start(bf16[256,256]{1,0:T(8,128)(2,1)} %param.24) | copy-start | bytes 393220
  102.1 84.9 %copy-start.3 = (f32[256]{0:T(256)S(1)}, f32[256]{0:T(256)}, u32[]{:S(2)}) copy-start(f32[256]{0:T(256)} %param.25) | copy-start | bytes 3076
  102.1 85.5 %copy-start.6 = (bf16[256,1024]{1,0:T(8,128)(2,1)S(1)}, bf16[256,1024]{1,0:T(8,128)(2,1)}, u32[]{:S(2)}) copy-start(bf16[256,1024]{1,0:T(8,128)(2,1)} %param.28) | copy-start | bytes 1572868
  102.1 85.5 %copy-start.7 = (f32[1024]{0:T(1024)S(1)}, f32[1024]{0:T(1024)}, u32[]{:S(2)}) copy-start(f32[1024]{0:T(1024)} %param.29) | copy-start | bytes 12292
  102.1 85.5 %copy-start.8 = (f32[256]{0:T(256)S(1)}, f32[256]{0:T(256)}, u32[]{:S(2)}) copy-start(f32[256]{0:T(256)} %param.31) | copy-start | bytes 3076
  102.2 85.5 %copy-start.9 = (f32[256]{0:T(256)S(1)}, f32[256]{0:T(256)}, u32[]{:S(2)}) copy-start(f32[256]{0:T(256)} %param.27) | copy-start | bytes 3076
  102.2 85.5 %copy-start.10 = (f32[256]{0:T(256)S(1)}, f32[256]{0:T(256)}, u32[]{:S(2)}) copy-start(f32[256]{0:T(256)} %param.26) | copy-start | bytes 3076
  102.2 86.3 %copy-start.4 = (f32[256]{0:T(256)S(1)}, f32[256]{0:T(256)}, u32[]{:S(2)}) copy-start(f32[256]{0:T(256)} %param.33) | copy-start | bytes 3076
  102.2 86.3 %copy-start.5 = (f32[256]{0:T(256)S(1)}, f32[256]{0:T(256)}, u32[]{:S(2)}) copy-start(f32[256]{0:T(256)} %param.32) | copy-start | bytes 3076
Sparse Core Ops, SparseCore 0:
  20.9 59.3 all-gather.3
where the time goes:
time: 197 us; the launch traced here: 196 us
  matrix products  74.4 us (38%)
  waiting for transfers between devices  55 us (28%)
  local copies, waits for them, and re-layouts  36.6 us (19%)
  between operations  13.6 us (7%)
  blocking collectives  13 us (7%)
  other arithmetic  3.03 us (2%)
    all_gather x1, waiting for transfers between devices, stacked_from(): pieces = lax.all_gather(pieces, axes[k], axis=0, tiled=True)  55 us
    dot_general x8, matrix products, one_head(): jnp.einsum('qsa,qsb->qab', group_hits, lane_hits, preferred_element_type=...  31.6 us
    dot_general x8, matrix products, one_head(): jnp.einsum('qab,abd->qd', table_minor, value_one, preferred_element_type=...  20.3 us
    dot_general x8, matrix products, one_head(): jnp.einsum('qab,abd->qd', table_major, value_one, preferred_element_type=...  20.3 us
    unnamed x28, local copies, waits for them, and re-layouts  15.5 us
    all_gather x1, blocking collectives, stacked_from(): pieces = lax.all_gather(pieces, axes[k], axis=0, tiled=True)  13 us
    dynamic_slice x40, local copies, waits for them, and re-layouts, blend_rows(): blended = lax.map(one_head, (place_heads, weight_heads, per_head))  11.1 us
    another operation x1, local copies, waits for them, and re-layouts, joined_along(): pieces.reshape(*dims[:dim], dims[dim] * dims[dim + 1], *dims[dim + 2:])  5.19 us
  transfers between devices with their start and end apart: 1, of which 1 were waited for; matrix products, arithmetic and copies ran while one was open for 2% of the time, Pallas kernels for 0%

commit v1 on v0

--- a/solution.py
+++ b/solution.py
@@ -10,6 +10,10 @@
 ROWS_DEV = 192
 BAND = ("band_0", "band_1")
 DP_BAND = ("dp", "band_0", "band_1")
+_draw_roots = lambda view, row_axis: jnp.concatenate(
+    lax.all_to_all(jnp.stack([view for _ in range(lax.axis_size(row_axis))]), row_axis, 0, 0),
+    axis=0,
+)
 
 
 def joined_along(pieces, dim):
@@ -21,7 +25,7 @@
 def stacked_from(shard, axes, order):
     pieces = shard[None]
     for k in order:
-        pieces = lax.all_gather(pieces, axes[k], axis=0, tiled=True)
+        pieces = _draw_roots(pieces, axes[k])
     held = [lax.axis_size(axes[k]) for k in reversed(order)]
     pieces = pieces.reshape(*held, *shard.shape)
     turned = sorted(range(len(order)), key=lambda place: order[len(order) - 1 - place])

time: 197 us -> 235 us (1.19)
  waiting for transfers between devices: 55 us -> 94.9 us
  between operations: 13.6 us -> 0.27 us
  starting transfers between devices: 0.01 us -> 8.31 us
  local copies, waits for them, and re-layouts: 36.6 us -> 39.6 us
    all_to_all x0 -> x1, waiting for transfers between devices: none -> 94.9 us  [lax.all_to_all(jnp.stack([view for _ in range(lax.axis_size(row_axis))]),...]
    all_gather x1 -> x0, waiting for transfers between devices: 55 us -> none  [stacked_from(): pieces = lax.all_gather(pieces, axes[k], axis=0, tiled=True)]
    all_to_all x0 -> x1, blocking collectives: none -> 13.4 us  [lax.all_to_all(jnp.stack([view for _ in range(lax.axis_size(row_axis))]),...]
    all_gather x1 -> x0, blocking collectives: 13 us -> none  [stacked_from(): pieces = lax.all_gather(pieces, axes[k], axis=0, tiled=True)]
    unnamed x28 -> x35, local copies, waits for them, and re-layouts: 15.5 us -> 24.9 us
    all_to_all x0 -> x1, starting transfers between devices: none -> 8.31 us  [lax.all_to_all(jnp.stack([view for _ in range(lax.axis_size(row_axis))]),...]
    reshape x1 -> x0, local copies, waits for them, and re-layouts: 4.61 us -> none  [stacked_from(): pieces = pieces.reshape(*held, *shard.shape)]
    another operation x1 -> x3, local copies, waits for them, and re-layouts: 5.19 us -> 3.46 us  [jnp.stack([view for _ in range(lax.axis_size(row_axis))])]
  transfers between devices with their start and end apart: 1 -> 1, of which waited for: 1 -> 1; matrix products, arithmetic and copies ran while one was open for 2% -> 1% of each run, Pallas kernels for 0% -> 0%
where the time goes in v1:
time: 235 us; the launch traced here: 234 us
  waiting for transfers between devices  94.9 us (40%)
  matrix products  74.4 us (32%)
  local copies, waits for them, and re-layouts  39.6 us (17%)
  blocking collectives  13.4 us (6%)
  starting transfers between devices  8.31 us (4%)
  other arithmetic  3.02 us (1%)
    all_to_all x1, waiting for transfers between devices, lax.all_to_all(jnp.stack([view for _ in range(lax.axis_size(row_axis))]),...  94.9 us
    dot_general x8, matrix products, one_head(): jnp.einsum('qsa,qsb->qab', group_hits, lane_hits, preferred_element_type=...  31.6 us
    unnamed x35, local copies, waits for them, and re-layouts  24.9 us
    dot_general x8, matrix products, one_head(): jnp.einsum('qab,abd->qd', table_minor, value_one, preferred_element_type=...  20.3 us
    dot_general x8, matrix products, one_head(): jnp.einsum('qab,abd->qd', table_major, value_one, preferred_element_type=...  20.3 us
    all_to_all x1, blocking collectives, lax.all_to_all(jnp.stack([view for _ in range(lax.axis_size(row_axis))]),...  13.4 us
    dynamic_slice x40, local copies, waits for them, and re-layouts, blend_rows(): blended = lax.map(one_head, (place_heads, weight_heads, per_head))  11.1 us
    all_to_all x1, starting transfers between devices, lax.all_to_all(jnp.stack([view for _ in range(lax.axis_size(row_axis))]),...  8.31 us
  transfers between devices with their start and end apart: 1, of which 1 were waited for; matrix products, arithmetic and copies ran while one was open for 1% of the time, Pallas kernels for 0%

profile of v1, /device:TPU:1, one launch (start us, length us, event | category | flops | bytes accessed | tf_op | source)
XLA Modules:
  0.0 234.5 jit_solution(12295577622277977156)
XLA Ops:
  0.0 1.2 fusion.40
  1.3 13.4 %all_to_all.10 = bf16[4,1,255,256]{3,2,1,0:T(8,128)(2,1)S(1)} all-to-all(bf16[4,1,255,256]{3,2,1,0:T(8,128)(2,1)S(1)} %stack.14), channel_id=1, replica_groups=mesh['dp'=8,'band_0'=4,'band_1'=8] {'band_0'}, dimensions={0} | all-to-all | bytes 1044480 | tf_op jit(solution)/shard_map/all_to_all | solution.py:14
  14.7 0.4 copy.42
  15.1 3.0 %stack.15 = bf16[8,4,255,256]{3,1,2,0:T(4,128)(2,1)} broadcast(bf16[4,255,256]{2,0,1:T(4,128)(2,1)S(1)} %copy.42), dimensions={1,2,3} | broadcast | bytes 4700160 | tf_op jit(solution)/shard_map/stack | solution.py:14
  18.1 8.3 %all-to-all-start.1 = ((bf16[8,4,255,256]{3,1,2,0:T(4,128)(2,1)}), bf16[8,4,255,256]{3,1,2,0:T(4,128)(2,1)}, u32[]{:S(2)}, u32[]{:S(2)}) async-start(bf16[8,4,255,256]{3,1,2,0:T(4,128)(2,1)} %stack.15), calls=%async_computation.1 | async-start | bytes 8355840 | tf_op jit(solution)/shard_map/all_to_all | solution.py:14
  27.1 0.3 fusion.41
  27.4 0.5 fusion.45
  28.0 94.9 %all-to-all-done.1 = bf16[8,4,255,256]{3,1,2,0:T(4,128)(2,1)} async-done(((bf16[8,4,255,256]{3,1,2,0:T(4,128)(2,1)}), bf16[8,4,255,256]{3,1,2,0:T(4,128)(2,1)}, u32[]{:S(2)}, u32[]{:S(2)}) %all-to-all-start.1) | async-done | bytes 4177952 | tf_op jit(solution)/shard_map/all_to_all | solution.py:14
  122.9 9.0 %copy.52 = bf16[4,8,255,256]{2,1,0,3:T(8,128)(2,1)} copy(bf16[4,8,255,256]{3,0,2,1:T(4,128)(2,1)} %bitcast.7) | data formatting | bytes 8355840
  131.9 9.7 %reshape.115 = bf16[8160,256]{0,1:T(8,128)(2,1)} reshape(bf16[4,8,255,256]{2,1,0,3:T(8,128)(2,1)} %copy.52) | data formatting | bytes 8355840
  141.6 2.5 %pad_bitcast_fusion = bf16[32,8,64,128]{3,1,2,0:T(8,128)(2,1)S(1)} fusion(bf16[8160,256]{0,1:T(8,128)(2,1)} %reshape.115), kind=kLoop, calls=%fused_computation.35 | loop fusion | bytes 8372224
  144.1 3.1 %copy.54 = bf16[32,8,64,128]{3,2,1,0:T(8,128)(2,1)} copy(bf16[32,8,64,128]{3,1,2,0:T(8,128)(2,1)S(1)} %pad_bitcast_fusion) | data formatting | bytes 8388608
  147.4 84.8 %while.13 = (s32[]{:T(128)}, bf16[8,255,32]{1,2,0:T(8,128)(2,1)S(1)}, s32[8,255,64]{1,2,0:T(8,128)S(1)}, bf16[8,255,64]{1,0,2:T(8,128)(2,1)S(1)}, bf16[8,64,128,32]{2,1,3,0:T(8,128)(2,1)}, /*index=5*/s32[]{:T(128)}) while((s32[]{:T(128)}, bf16[8,255,32]{1,2,0:T(8,128)(2,1)S(1)}, s32[8,255,64]{1,2,0:T(8,128)S(1)}, ...), condition=%wide.region_1.2_spmd.clone, body=%wide.region_0.1_spmd.clone.sunk | while | flops 547625728 | bytes 19657812 | solution.py:77
  147.8 4.0 %subtract_convert_fusion.2 = (bf16[255,64,128]{2,1,0:T(8,128)(2,1)S(1)}, bf16[255,64,128]{2,1,0:T(8,128)(2,1)S(1)}) fusion(s32[255,64]{1,0:T(8,128)S(1)} %get-tuple-element.178, s32[255,64]{1,0:T(8,128)S(1)} %get-tuple-element.179, bf16[255,64]{1,0:T(8,128)(2,1)S(1)} %bitcast.98), kind=kOutput, calls=%fused_computation.4.clone.1 | convolution fusion | flops 279920640 | bytes 8519040 | tf_op jit(solution)/shard_map/while/body/eval_jaxpr/qsa,qsb->qab/dot_general | solution.py:64
  151.8 1.1 constant_dynamic-slice_fusion.8
  152.9 2.5 %fusion.82 = f32[255,32]{0,1:T(8,128)S(1)} fusion(bf16[255,64,128]{2,1,0:T(8,128)(2,1)S(1)} %get-tuple-element.180, bf16[1,64,128,32]{2,1,3,0:T(8,128)(2,1)S(1)} %constant_dynamic-slice_fusion.8), kind=kOutput, calls=%fused_computation.15.clone.1 | convolution fusion | flops 133693440 | bytes 4734848 | tf_op jit(solution)/shard_map/while/body/eval_jaxpr/qab,abd->qd/dot_general | solution.py:69
  155.4 2.5 %fusion.83 = bf16[8,255,32]{1,2,0:T(8,128)(2,1)S(1)} fusion(bf16[8,255,32]{1,2,0:T(8,128)(2,1)S(1)} %get-tuple-element.189, s32[]{:T(128)} %get-tuple-element.188, f32[255,32]{0,1:T(8,128)S(1)} %fusion.82, bf16[255,64,128]{2,1,0:T(8,128)(2,1)S(1)} %get-tuple-element.181, bf16[1,64,128,32]{2,1,3,0:T(8,128)(2,1)S(1)} %constant_dynamic-slice_fusion.8), kind=kOutput, calls=%fused_computation.19.clone.1 | convolution fusion | flops 133701600 | bytes 4767748 | tf_op jit(solution)/shard_map/while/body/eval_jaxpr/qab,abd->qd/dot_general | solution.py:72
  158.4 4.0 %subtract_convert_fusion.2 = (bf16[255,64,128]{2,1,0:T(8,128)(2,1)S(1)}, bf16[255,64,128]{2,1,0:T(8,128)(2,1)S(1)}) fusion(s32[255,64]{1,0:T(8,128)S(1)} %get-tuple-element.178, s32[255,64]{1,0:T(8,128)S(1)} %get-tuple-element.179, bf16[255,64]{1,0:T(8,128)(2,1)S(1)} %bitcast.98), kind=kOutput, calls=%fused_computation.4.clone.1 | convolution fusion | flops 279920640 | bytes 8519040 | tf_op jit(solution)/shard_map/while/body/eval_jaxpr/qsa,qsb->qab/dot_general | solution.py:64
  162.4 1.1 constant_dynamic-slice_fusion.8
  163.5 2.5 %fusion.82 = f32[255,32]{0,1:T(8,128)S(1)} fusion(bf16[255,64,128]{2,1,0:T(8,128)(2,1)S(1)} %get-tuple-element.180, bf16[1,64,128,32]{2,1,3,0:T(8,128)(2,1)S(1)} %constant_dynamic-slice_fusion.8), kind=kOutput, calls=%fused_computation.15.clone.1 | convolution fusion | flops 133693440 | bytes 4734848 | tf_op jit(solution)/shard_map/while/body/eval_jaxpr/qab,abd->qd/dot_general | solution.py:69
  166.0 2.5 %fusion.83 = bf16[8,255,32]{1,2,0:T(8,128)(2,1)S(1)} fusion(bf16[8,255,32]{1,2,0:T(8,128)(2,1)S(1)} %get-tuple-element.189, s32[]{:T(128)} %get-tuple-element.188, f32[255,32]{0,1:T(8,128)S(1)} %fusion.82, bf16[255,64,128]{2,1,0:T(8,128)(2,1)S(1)} %get-tuple-element.181, bf16[1,64,128,32]{2,1,3,0:T(8,128)(2,1)S(1)} %constant_dynamic-slice_fusion.8), kind=kOutput, calls=%fused_computation.19.clone.1 | convolution fusion | flops 133701600 | bytes 4767748 | tf_op jit(solution)/shard_map/while/body/eval_jaxpr/qab,abd->qd/dot_general | solution.py:72
  169.0 4.0 %subtract_convert_fusion.2 = (bf16[255,64,128]{2,1,0:T(8,128)(2,1)S(1)}, bf16[255,64,128]{2,1,0:T(8,128)(2,1)S(1)}) fusion(s32[255,64]{1,0:T(8,128)S(1)} %get-tuple-element.178, s32[255,64]{1,0:T(8,128)S(1)} %get-tuple-element.179, bf16[255,64]{1,0:T(8,128)(2,1)S(1)} %bitcast.98), kind=kOutput, calls=%fused_computation.4.clone.1 | convolution fusion | flops 279920640 | bytes 8519040 | tf_op jit(solution)/shard_map/while/body/eval_jaxpr/qsa,qsb->qab/dot_general | solution.py:64
  173.0 1.1 constant_dynamic-slice_fusion.8
  174.1 2.5 %fusion.82 = f32[255,32]{0,1:T(8,128)S(1)} fusion(bf16[255,64,128]{2,1,0:T(8,128)(2,1)S(1)} %get-tuple-element.180, bf16[1,64,128,32]{2,1,3,0:T(8,128)(2,1)S(1)} %constant_dynamic-slice_fusion.8), kind=kOutput, calls=%fused_computation.15.clone.1 | convolution fusion | flops 133693440 | bytes 4734848 | tf_op jit(solution)/shard_map/while/body/eval_jaxpr/qab,abd->qd/dot_general | solution.py:69
  176.6 2.5 %fusion.83 = bf16[8,255,32]{1,2,0:T(8,128)(2,1)S(1)} fusion(bf16[8,255,32]{1,2,0:T(8,128)(2,1)S(1)} %get-tuple-element.189, s32[]{:T(128)} %get-tuple-element.188, f32[255,32]{0,1:T(8,128)S(1)} %fusion.82, bf16[255,64,128]{2,1,0:T(8,128)(2,1)S(1)} %get-tuple-element.181, bf16[1,64,128,32]{2,1,3,0:T(8,128)(2,1)S(1)} %constant_dynamic-slice_fusion.8), kind=kOutput, calls=%fused_computation.19.clone.1 | convolution fusion | flops 133701600 | bytes 4767748 | tf_op jit(solution)/shard_map/while/body/eval_jaxpr/qab,abd->qd/dot_general | solution.py:72
  179.6 3.9 %subtract_convert_fusion.2 = (bf16[255,64,128]{2,1,0:T(8,128)(2,1)S(1)}, bf16[255,64,128]{2,1,0:T(8,128)(2,1)S(1)}) fusion(s32[255,64]{1,0:T(8,128)S(1)} %get-tuple-element.178, s32[255,64]{1,0:T(8,128)S(1)} %get-tuple-element.179, bf16[255,64]{1,0:T(8,128)(2,1)S(1)} %bitcast.98), kind=kOutput, calls=%fused_computation.4.clone.1 | convolution fusion | flops 279920640 | bytes 8519040 | tf_op jit(solution)/shard_map/while/body/eval_jaxpr/qsa,qsb->qab/dot_general | solution.py:64
  183.6 1.1 constant_dynamic-slice_fusion.8
  184.7 2.5 %fusion.82 = f32[255,32]{0,1:T(8,128)S(1)} fusion(bf16[255,64,128]{2,1,0:T(8,128)(2,1)S(1)} %get-tuple-element.180, bf16[1,64,128,32]{2,1,3,0:T(8,128)(2,1)S(1)} %constant_dynamic-slice_fusion.8), kind=kOutput, calls=%fused_computation.15.clone.1 | convolution fusion | flops 133693440 | bytes 4734848 | tf_op jit(solution)/shard_map/while/body/eval_jaxpr/qab,abd->qd/dot_general | solution.py:69
  187.2 2.5 %fusion.83 = bf16[8,255,32]{1,2,0:T(8,128)(2,1)S(1)} fusion(bf16[8,255,32]{1,2,0:T(8,128)(2,1)S(1)} %get-tuple-element.189, s32[]{:T(128)} %get-tuple-element.188, f32[255,32]{0,1:T(8,128)S(1)} %fusion.82, bf16[255,64,128]{2,1,0:T(8,128)(2,1)S(1)} %get-tuple-element.181, bf16[1,64,128,32]{2,1,3,0:T(8,128)(2,1)S(1)} %constant_dynamic-slice_fusion.8), kind=kOutput, calls=%fused_computation.19.clone.1 | convolution fusion | flops 133701600 | bytes 4767748 | tf_op jit(solution)/shard_map/while/body/eval_jaxpr/qab,abd->qd/dot_general | solution.py:72
  190.2 4.0 %subtract_convert_fusion.2 = (bf16[255,64,128]{2,1,0:T(8,128)(2,1)S(1)}, bf16[255,64,128]{2,1,0:T(8,128)(2,1)S(1)}) fusion(s32[255,64]{1,0:T(8,128)S(1)} %get-tuple-element.178, s32[255,64]{1,0:T(8,128)S(1)} %get-tuple-element.179, bf16[255,64]{1,0:T(8,128)(2,1)S(1)} %bitcast.98), kind=kOutput, calls=%fused_computation.4.clone.1 | convolution fusion | flops 279920640 | bytes 8519040 | tf_op jit(solution)/shard_map/while/body/eval_jaxpr/qsa,qsb->qab/dot_general | solution.py:64
  194.2 1.1 constant_dynamic-slice_fusion.8
  195.3 2.5 %fusion.82 = f32[255,32]{0,1:T(8,128)S(1)} fusion(bf16[255,64,128]{2,1,0:T(8,128)(2,1)S(1)} %get-tuple-element.180, bf16[1,64,128,32]{2,1,3,0:T(8,128)(2,1)S(1)} %constant_dynamic-slice_fusion.8), kind=kOutput, calls=%fused_computation.15.clone.1 | convolution fusion | flops 133693440 | bytes 4734848 | tf_op jit(solution)/shard_map/while/body/eval_jaxpr/qab,abd->qd/dot_general | solution.py:69
  197.8 2.5 %fusion.83 = bf16[8,255,32]{1,2,0:T(8,128)(2,1)S(1)} fusion(bf16[8,255,32]{1,2,0:T(8,128)(2,1)S(1)} %get-tuple-element.189, s32[]{:T(128)} %get-tuple-element.188, f32[255,32]{0,1:T(8,128)S(1)} %fusion.82, bf16[255,64,128]{2,1,0:T(8,128)(2,1)S(1)} %get-tuple-element.181, bf16[1,64,128,32]{2,1,3,0:T(8,128)(2,1)S(1)} %constant_dynamic-slice_fusion.8), kind=kOutput, calls=%fused_computation.19.clone.1 | convolution fusion | flops 133701600 | bytes 4767748 | tf_op jit(solution)/shard_map/while/body/eval_jaxpr/qab,abd->qd/dot_general | solution.py:72
  200.9 4.0 %subtract_convert_fusion.2 = (bf16[255,64,128]{2,1,0:T(8,128)(2,1)S(1)}, bf16[255,64,128]{2,1,0:T(8,128)(2,1)S(1)}) fusion(s32[255,64]{1,0:T(8,128)S(1)} %get-tuple-element.178, s32[255,64]{1,0:T(8,128)S(1)} %get-tuple-element.179, bf16[255,64]{1,0:T(8,128)(2,1)S(1)} %bitcast.98), kind=kOutput, calls=%fused_computation.4.clone.1 | convolution fusion | flops 279920640 | bytes 8519040 | tf_op jit(solution)/shard_map/while/body/eval_jaxpr/qsa,qsb->qab/dot_general | solution.py:64
  204.8 1.1 constant_dynamic-slice_fusion.8
  205.9 2.5 %fusion.82 = f32[255,32]{0,1:T(8,128)S(1)} fusion(bf16[255,64,128]{2,1,0:T(8,128)(2,1)S(1)} %get-tuple-element.180, bf16[1,64,128,32]{2,1,3,0:T(8,128)(2,1)S(1)} %constant_dynamic-slice_fusion.8), kind=kOutput, calls=%fused_computation.15.clone.1 | convolution fusion | flops 133693440 | bytes 4734848 | tf_op jit(solution)/shard_map/while/body/eval_jaxpr/qab,abd->qd/dot_general | solution.py:69
  208.4 2.5 %fusion.83 = bf16[8,255,32]{1,2,0:T(8,128)(2,1)S(1)} fusion(bf16[8,255,32]{1,2,0:T(8,128)(2,1)S(1)} %get-tuple-element.189, s32[]{:T(128)} %get-tuple-element.188, f32[255,32]{0,1:T(8,128)S(1)} %fusion.82, bf16[255,64,128]{2,1,0:T(8,128)(2,1)S(1)} %get-tuple-element.181, bf16[1,64,128,32]{2,1,3,0:T(8,128)(2,1)S(1)} %constant_dynamic-slice_fusion.8), kind=kOutput, calls=%fused_computation.19.clone.1 | convolution fusion | flops 133701600 | bytes 4767748 | tf_op jit(solution)/shard_map/while/body/eval_jaxpr/qab,abd->qd/dot_general | solution.py:72
  211.5 4.0 %subtract_convert_fusion.2 = (bf16[255,64,128]{2,1,0:T(8,128)(2,1)S(1)}, bf16[255,64,128]{2,1,0:T(8,128)(2,1)S(1)}) fusion(s32[255,64]{1,0:T(8,128)S(1)} %get-tuple-element.178, s32[255,64]{1,0:T(8,128)S(1)} %get-tuple-element.179, bf16[255,64]{1,0:T(8,128)(2,1)S(1)} %bitcast.98), kind=kOutput, calls=%fused_computation.4.clone.1 | convolution fusion | flops 279920640 | bytes 8519040 | tf_op jit(solution)/shard_map/while/body/eval_jaxpr/qsa,qsb->qab/dot_general | solution.py:64
  215.4 1.1 constant_dynamic-slice_fusion.8
  216.5 2.5 %fusion.82 = f32[255,32]{0,1:T(8,128)S(1)} fusion(bf16[255,64,128]{2,1,0:T(8,128)(2,1)S(1)} %get-tuple-element.180, bf16[1,64,128,32]{2,1,3,0:T(8,128)(2,1)S(1)} %constant_dynamic-slice_fusion.8), kind=kOutput, calls=%fused_computation.15.clone.1 | convolution fusion | flops 133693440 | bytes 4734848 | tf_op jit(solution)/shard_map/while/body/eval_jaxpr/qab,abd->qd/dot_general | solution.py:69
  219.0 2.5 %fusion.83 = bf16[8,255,32]{1,2,0:T(8,128)(2,1)S(1)} fusion(bf16[8,255,32]{1,2,0:T(8,128)(2,1)S(1)} %get-tuple-element.189, s32[]{:T(128)} %get-tuple-element.188, f32[255,32]{0,1:T(8,128)S(1)} %fusion.82, bf16[255,64,128]{2,1,0:T(8,128)(2,1)S(1)} %get-tuple-element.181, bf16[1,64,128,32]{2,1,3,0:T(8,128)(2,1)S(1)} %constant_dynamic-slice_fusion.8), kind=kOutput, calls=%fused_computation.19.clone.1 | convolution fusion | flops 133701600 | bytes 4767748 | tf_op jit(solution)/shard_map/while/body/eval_jaxpr/qab,abd->qd/dot_general | solution.py:72
  222.1 3.9 %subtract_convert_fusion.2 = (bf16[255,64,128]{2,1,0:T(8,128)(2,1)S(1)}, bf16[255,64,128]{2,1,0:T(8,128)(2,1)S(1)}) fusion(s32[255,64]{1,0:T(8,128)S(1)} %get-tuple-element.178, s32[255,64]{1,0:T(8,128)S(1)} %get-tuple-element.179, bf16[255,64]{1,0:T(8,128)(2,1)S(1)} %bitcast.98), kind=kOutput, calls=%fused_computation.4.clone.1 | convolution fusion | flops 279920640 | bytes 8519040 | tf_op jit(solution)/shard_map/while/body/eval_jaxpr/qsa,qsb->qab/dot_general | solution.py:64
  226.0 1.1 constant_dynamic-slice_fusion.8
  227.1 2.5 %fusion.82 = f32[255,32]{0,1:T(8,128)S(1)} fusion(bf16[255,64,128]{2,1,0:T(8,128)(2,1)S(1)} %get-tuple-element.180, bf16[1,64,128,32]{2,1,3,0:T(8,128)(2,1)S(1)} %constant_dynamic-slice_fusion.8), kind=kOutput, calls=%fused_computation.15.clone.1 | convolution fusion | flops 133693440 | bytes 4734848 | tf_op jit(solution)/shard_map/while/body/eval_jaxpr/qab,abd->qd/dot_general | solution.py:69
  229.6 2.5 %fusion.83 = bf16[8,255,32]{1,2,0:T(8,128)(2,1)S(1)} fusion(bf16[8,255,32]{1,2,0:T(8,128)(2,1)S(1)} %get-tuple-element.189, s32[]{:T(128)} %get-tuple-element.188, f32[255,32]{0,1:T(8,128)S(1)} %fusion.82, bf16[255,64,128]{2,1,0:T(8,128)(2,1)S(1)} %get-tuple-element.181, bf16[1,64,128,32]{2,1,3,0:T(8,128)(2,1)S(1)} %constant_dynamic-slice_fusion.8), kind=kOutput, calls=%fused_computation.19.clone.1 | convolution fusion | flops 133701600 | bytes 4767748 | tf_op jit(solution)/shard_map/while/body/eval_jaxpr/qab,abd->qd/dot_general | solution.py:72
  232.2 0.3 fusion.68
  232.8 0.7 fusion.69
  233.7 0.8 add_convert_fusion
  (82 shorter events, 4.6 us)
Async XLA Ops:
  0.0 232.7 %copy-start = (bf16[1024,256]{1,0:T(8,128)(2,1)S(1)}, bf16[1024,256]{1,0:T(8,128)(2,1)}, u32[]{:S(2)}) copy-start(bf16[1024,256]{1,0:T(8,128)(2,1)} %param.30) | copy-start | bytes 1572868
  18.1 8.3 %copy-start.2 = (s32[255,512]{1,0:T(8,128)S(1)}, s32[255,512]{1,0:T(8,128)}, u32[]{:S(2)}) copy-start(s32[255,512]{1,0:T(8,128)} %param.19) | copy-start | bytes 1566724
  18.1 8.5 %copy-start.3 = (f32[255,512]{1,0:T(8,128)S(1)}, f32[255,512]{1,0:T(8,128)}, u32[]{:S(2)}) copy-start(f32[255,512]{1,0:T(8,128)} %param.20) | copy-start | bytes 1566724
  18.1 8.7 %copy-start.5 = (f32[255,128]{1,0:T(8,128)S(1)}, f32[255,128]{1,0:T(8,128)}, u32[]{:S(2)}) copy-start(f32[255,128]{1,0:T(8,128)} %param.21) | copy-start | bytes 391684
  18.1 104.8 %all-to-all-start.1 = ((bf16[8,4,255,256]{3,1,2,0:T(4,128)(2,1)}), bf16[8,4,255,256]{3,1,2,0:T(4,128)(2,1)}, u32[]{:S(2)}, u32[]{:S(2)}) async-start(bf16[8,4,255,256]{3,1,2,0:T(4,128)(2,1)} %stack.15), calls=%async_computation.1 | async-start | bytes 8355840 | tf_op jit(solution)/shard_map/all_to_all | solution.py:14
  147.3 84.9 %copy-start.1 = (bf16[255,256]{1,0:T(8,128)(2,1)S(1)}, bf16[255,256]{1,0:T(8,128)(2,1)}, u32[]{:S(2)}) copy-start(bf16[255,256]{1,0:T(8,128)(2,1)} %param.18) | copy-start | bytes 391684
  147.3 84.9 %copy-start.4 = (bf16[256,256]{1,0:T(8,128)(2,1)S(1)}, bf16[256,256]{1,0:T(8,128)(2,1)}, u32[]{:S(2)}) copy-start(bf16[256,256]{1,0:T(8,128)(2,1)} %param.24) | copy-start | bytes 393220
  147.3 84.9 %copy-start.6 = (f32[256]{0:T(256)S(1)}, f32[256]{0:T(256)}, u32[]{:S(2)}) copy-start(f32[256]{0:T(256)} %param.25) | copy-start | bytes 3076
  147.3 85.5 %copy-start.9 = (bf16[256,1024]{1,0:T(8,128)(2,1)S(1)}, bf16[256,1024]{1,0:T(8,128)(2,1)}, u32[]{:S(2)}) copy-start(bf16[256,1024]{1,0:T(8,128)(2,1)} %param.28) | copy-start | bytes 1572868
  147.3 85.5 %copy-start.10 = (f32[1024]{0:T(1024)S(1)}, f32[1024]{0:T(1024)}, u32[]{:S(2)}) copy-start(f32[1024]{0:T(1024)} %param.29) | copy-start | bytes 12292
  147.3 85.5 %copy-start.11 = (f32[256]{0:T(256)S(1)}, f32[256]{0:T(256)}, u32[]{:S(2)}) copy-start(f32[256]{0:T(256)} %param.31) | copy-start | bytes 3076
  147.3 85.5 %copy-start.12 = (f32[256]{0:T(256)S(1)}, f32[256]{0:T(256)}, u32[]{:S(2)}) copy-start(f32[256]{0:T(256)} %param.27) | copy-start | bytes 3076
  147.3 85.5 %copy-start.13 = (f32[256]{0:T(256)S(1)}, f32[256]{0:T(256)}, u32[]{:S(2)}) copy-start(f32[256]{0:T(256)} %param.26) | copy-start | bytes 3076
  147.3 86.3 %copy-start.7 = (f32[256]{0:T(256)S(1)}, f32[256]{0:T(256)}, u32[]{:S(2)}) copy-start(f32[256]{0:T(256)} %param.33) | copy-start | bytes 3076
  147.4 86.3 %copy-start.8 = (f32[256]{0:T(256)S(1)}, f32[256]{0:T(256)}, u32[]{:S(2)}) copy-start(f32[256]{0:T(256)} %param.32) | copy-start | bytes 3076
